TPU v7x, 32 devices: a whole 2x2x4 slice. The times are simulated.
32 devices in a mesh: group: 4 (over y, core), rep: 8 (over z, x).
Axes of the slice: x: 2, y: 2, z: 4, core: 2. Of those that a mesh axis runs over, the one named last changes fastest.
Arguments:
- table_hot: bfloat16 [32768, 512], P(('group', 'rep')), may hold values from -6 to 6
- table_mid: bfloat16 [131072, 128], P(('group', 'rep')), may hold values from -6 to 6
- table_cold: bfloat16 [131072, 128], P(('group', 'rep')), may hold values from -6 to 6
- proj_hot: bfloat16 [512, 256], replicated, may hold values from -0.25 to 0.25
- proj_mid: bfloat16 [128, 256], replicated, may hold values from -0.5 to 0.5
- proj_cold: bfloat16 [32, 256], replicated, may hold values from -1 to 1
- tower_in: bfloat16 [256, 1024], replicated, may hold values from -0.375 to 0.375
- tower_out: bfloat16 [1024, 256], replicated, may hold values from -0.1875 to 0.1875
- queries: bfloat16 [16384, 256], P(('group', 'rep')), may hold values from -68 to 68
- labels: int32 [16384], P(('group', 'rep')), may hold values from 0 to 4095
- item_slot: int32 [32, 4, 1024], P(('group', 'rep')), may hold values from 0 to 255
- item_block: int32 [32, 4, 1024], P(('group', 'rep')), may hold values from 0 to 2
- serve_rows: int32 [32, 3, 256], P(('group', 'rep')), may hold values from 0 to 16383, as said below
Outputs:
- query_loss: float32 [16384], P(('group', 'rep'))
- query_grad: float32 [16384, 256], P(('group', 'rep'))
- grad_hot: float32 [32768, 512], P(('group', 'rep'))
- grad_mid: float32 [131072, 128], P(('group', 'rep'))
- grad_cold: float32 [131072, 128], P(('group', 'rep'))
- grad_proj_hot: float32 [512, 256], P(None, 'rep')
- grad_proj_mid: float32 [128, 256], P(None, 'rep')
- grad_proj_cold: float32 [32, 256], P(None, 'rep')
- grad_tower_in: float32 [256, 1024], P(None, 'rep')
- grad_tower_out: float32 [1024, 256], P(None, 'rep')
Inputs may be any that keep to these rules, and one draw needn't show every extreme that they name: serve_rows[o, b, d * 8 + c] is a row of owner o's shard of block b that requester d sees in slot c; for block 0 it is below 1024, for block 1 below 4096, for block 2 below 16384; the 8 rows that one owner serves to one requester in one block are distinct.
All inputs are finite; a program needn't handle non-finite values.
Results may differ from a plain program's by a relative error of at most 0.02.
The roundings to bfloat16 on the way count: a program that leaves them out, or rounds other values in their place, can miss the bound.
Values may be sent and summed in bfloat16 or wider, within the bound.
No kernel may reach another device: no remote copies, remote signals or barrier semaphores. Data moves between devices by JAX's collectives and lax.ppermute only.
A program may use at most 128 MiB of HBM per device.

v0:
```python
import jax
import jax.numpy as jnp
from jax import lax
from jax.sharding import PartitionSpec as P

NORM_EPS = 1e-06
LOGIT_SCALE = 0.2


def merged(value, axis, join):
    pieces = jax.tree.map(lambda part: lax.all_gather(part, axis), value)
    head = jax.tree.map(lambda part: part[0], pieces)
    tail = jax.tree.map(lambda part: part[1:], pieces)
    total, _ = lax.scan(lambda total, piece: (join(total, piece), None), head, tail)
    return total


def silu_slope(pre_act):
    sigmoid = jax.nn.sigmoid(pre_act)
    return sigmoid * (1.0 + pre_act * (1.0 - sigmoid))


def pick_cold(cold_lines, row_ids, col_width):
    pieces = cold_lines.reshape(cold_lines.shape[0], 4, col_width)
    select = lax.broadcasted_iota(jnp.int32, (row_ids.shape[0], 4), 1) == (row_ids % 4)[:, None]
    return jnp.sum(jnp.where(select[:, :, None], pieces, jnp.zeros((), pieces.dtype)), axis=1)


def cold_add(row_ids, values, line_shape):
    select = (
        lax.broadcasted_iota(jnp.int32, (row_ids.shape[0], 4), 1) == (row_ids % 4)[:, None]
    ).astype(jnp.float32)
    spread = (select[:, :, None] * values[:, None, :]).reshape(row_ids.shape[0], line_shape[1])
    return jnp.zeros(line_shape, jnp.float32).at[row_ids // 4].add(spread)


def project(raw_rows, weight):
    return jnp.dot(raw_rows, weight, preferred_element_type=jnp.float32).astype(jnp.bfloat16)


def unproject(slot_grad, weight):
    return lax.dot_general(
        slot_grad, weight, (((1,), (1,)), ((), ())), preferred_element_type=jnp.float32
    )


def contract(left_rows, right_rows):
    return lax.dot_general(
        left_rows, right_rows, (((0,), (0,)), ((), ())), preferred_element_type=jnp.float32
    )


def combine_totals(earlier, later):
    joint_max = jnp.maximum(earlier[0], later[0])
    joint_sum = earlier[1] * jnp.exp(earlier[0] - joint_max) + later[1] * jnp.exp(
        later[0] - joint_max
    )
    return (joint_max, joint_sum, earlier[2] + later[2])


def local(
    table_hot,
    table_mid,
    table_cold,
    proj_hot,
    proj_mid,
    proj_cold,
    tower_in,
    tower_out,
    queries,
    labels,
    item_slot,
    item_block,
    serve_rows,
):
    devices = lax.axis_size(("group", "rep"))
    served = serve_rows[0]
    slot_total = served.shape[1]
    slots_each = slot_total // devices
    cold_width = proj_cold.shape[0]
    width_model = tower_in.shape[0]
    item_count = item_slot.shape[2]
    field_count = item_slot.shape[1]
    rows_hot = table_hot[served[0]]
    rows_mid = table_mid[served[1]]
    rows_cold = pick_cold(table_cold[served[2] // 4], served[2], cold_width)
    first_block = rows_hot.reshape(devices, slots_each, rows_hot.shape[1])
    got_first, got_mid, got_cold = (
        lax.all_to_all(first_block, ("group", "rep"), split_axis=0, concat_axis=0, tiled=True),
        lax.all_to_all(
            rows_mid.reshape(devices, slots_each, rows_mid.shape[1]),
            ("group", "rep"),
            split_axis=0,
            concat_axis=0,
            tiled=True,
        ),
        lax.all_to_all(
            rows_cold.reshape(devices, slots_each // 4, 4 * cold_width),
            ("group", "rep"),
            split_axis=0,
            concat_axis=0,
            tiled=True,
        ),
    )
    raw_mid = got_mid.reshape(slot_total, rows_mid.shape[1])
    raw_cold = got_cold.reshape(slot_total, cold_width)
    raw_hot = got_first.reshape(slot_total, rows_hot.shape[1])
    near_hot = project(raw_hot, proj_hot)
    slot_table = jnp.concatenate(
        [near_hot, project(raw_mid, proj_mid), project(raw_cold, proj_cold)], axis=0
    )
    slot_index = item_block[0] * slot_total + item_slot[0]
    pooled = jnp.sum(slot_table[slot_index].astype(jnp.float32), axis=0).astype(jnp.bfloat16)
    pre_act = jnp.dot(pooled, tower_in, preferred_element_type=jnp.float32)
    hidden = jax.nn.silu(pre_act).astype(jnp.bfloat16)
    residual = pooled.astype(jnp.float32) + jnp.dot(
        hidden, tower_out, preferred_element_type=jnp.float32
    )
    inv_rms = lax.rsqrt(jnp.mean(residual * residual, axis=1, keepdims=True) + NORM_EPS)
    vectors = (residual * inv_rms).astype(jnp.bfloat16)
    group_queries = lax.all_gather(queries, "group", axis=0, tiled=True)
    group_labels = lax.all_gather(labels, "group", axis=0, tiled=True)
    scores = (
        lax.dot_general(
            group_queries, vectors, (((1,), (1,)), ((), ())), preferred_element_type=jnp.float32
        )
        * LOGIT_SCALE
    )
    group_at = lax.axis_index("group")
    columns = group_at * item_count + lax.broadcasted_iota(jnp.int32, scores.shape, 1)
    onehot = columns == group_labels[:, None]
    local_max = jnp.max(scores, axis=1)
    local_total = jnp.sum(jnp.exp(scores - local_max[:, None]), axis=1)
    local_pick = jnp.sum(jnp.where(onehot, scores, 0.0), axis=1)
    joint_max, joint_sum, picked = merged(
        (local_max, local_total, local_pick), "group", combine_totals
    )
    log_total = joint_max + jnp.log(joint_sum)
    score_grad = (jnp.exp(scores - log_total[:, None]) - onehot.astype(jnp.float32)).astype(
        jnp.bfloat16
    )
    vec_grad = LOGIT_SCALE * contract(score_grad, group_queries)
    query_grad = lax.psum_scatter(
        (LOGIT_SCALE * jnp.dot(score_grad, vectors, preferred_element_type=jnp.float32)).astype(
            jnp.bfloat16
        ),
        "group",
        scatter_dimension=0,
        tiled=True,
    ).astype(jnp.float32)
    query_loss = lax.dynamic_slice_in_dim(
        log_total - picked, group_at * queries.shape[0], queries.shape[0], 0
    )
    dot_wide = jnp.sum(vec_grad * residual, axis=1, keepdims=True)
    wide_grad = inv_rms * vec_grad - inv_rms**3 / width_model * residual * dot_wide
    wide_low = wide_grad.astype(jnp.bfloat16)
    hidden_grad = unproject(wide_low, tower_out)
    pre_grad = (hidden_grad * silu_slope(pre_act)).astype(jnp.bfloat16)
    pooled_grad = (unproject(pre_grad, tower_in) + wide_grad).astype(jnp.bfloat16)
    stacked = jnp.broadcast_to(
        pooled_grad.astype(jnp.float32)[None], (field_count, item_count, width_model)
    ).reshape(-1, width_model)
    slot_grad = jax.ops.segment_sum(
        stacked, slot_index.reshape(-1), num_segments=3 * slot_total
    ).astype(jnp.bfloat16)
    grad_hot_slots = slot_grad[:slot_total]
    grad_mid_slots = slot_grad[slot_total : 2 * slot_total]
    grad_cold_slots = slot_grad[2 * slot_total :]
    grad_ph = contract(raw_hot, grad_hot_slots)
    back_hot, back_mid, back_cold = (
        lax.all_to_all(
            unproject(grad_hot_slots, proj_hot)
            .reshape(devices, slots_each, rows_hot.shape[1])
            .astype(jnp.bfloat16),
            ("group", "rep"),
            split_axis=0,
            concat_axis=0,
            tiled=True,
        ).astype(jnp.float32),
        lax.all_to_all(
            unproject(grad_mid_slots, proj_mid)
            .reshape(devices, slots_each, rows_mid.shape[1])
            .astype(jnp.bfloat16),
            ("group", "rep"),
            split_axis=0,
            concat_axis=0,
            tiled=True,
        ).astype(jnp.float32),
        lax.all_to_all(
            unproject(grad_cold_slots, proj_cold)
            .reshape(devices, slots_each // 4, 4 * cold_width)
            .astype(jnp.bfloat16),
            ("group", "rep"),
            split_axis=0,
            concat_axis=0,
            tiled=True,
        ).astype(jnp.float32),
    )
    back_hot = back_hot.reshape(slot_total, rows_hot.shape[1])
    grad_pm = contract(raw_mid, grad_mid_slots)
    grad_pc = contract(raw_cold, grad_cold_slots)
    grad_hot = jnp.zeros(table_hot.shape, jnp.float32).at[served[0]].add(back_hot)
    grad_mid = (
        jnp.zeros(table_mid.shape, jnp.float32)
        .at[served[1]]
        .add(back_mid.reshape(slot_total, rows_mid.shape[1]))
    )
    grad_cold = cold_add(served[2], back_cold.reshape(slot_total, cold_width), table_cold.shape)
    grad_in_local = contract(pooled, pre_grad)
    grad_out_local = contract(hidden, wide_low)
    totals = lax.psum((grad_ph, grad_pm, grad_pc, grad_in_local, grad_out_local), ("group", "rep"))
    rep_count = lax.axis_size("rep")
    rep_at = lax.axis_index("rep")
    summed = tuple(
        (
            lax.dynamic_slice_in_dim(
                full_sum,
                rep_at * (full_sum.shape[1] // rep_count),
                full_sum.shape[1] // rep_count,
                1,
            )
            for full_sum in totals
        )
    )
    return (
        query_loss,
        query_grad,
        grad_hot,
        grad_mid,
        grad_cold,
        summed[0],
        summed[1],
        summed[2],
        summed[3],
        summed[4],
    )


def solution(mesh):
    return jax.shard_map(
        local,
        mesh=mesh,
        in_specs=(
            P(("group", "rep"), None),
            P(("group", "rep"), None),
            P(("group", "rep"), None),
            P(),
            P(),
            P(),
            P(),
            P(),
            P(("group", "rep"), None),
            P(("group", "rep")),
            P(("group", "rep"), None, None),
            P(("group", "rep"), None, None),
            P(("group", "rep"), None, None),
        ),
        out_specs=(
            P(("group", "rep")),
            P(("group", "rep"), None),
            P(("group", "rep"), None),
            P(("group", "rep"), None),
            P(("group", "rep"), None),
            P(None, "rep"),
            P(None, "rep"),
            P(None, "rep"),
            P(None, "rep"),
            P(None, "rep"),
        ),
        check_vma=False,
    )
```

profile of v0, /device:TPU:0, one launch (start us, length us, event | category | flops | bytes accessed | tf_op | source)
XLA Modules:
  0.0 317.9 jit_solution(5360440472956101922)
XLA Ops:
  9.4 2.1 gather_fusion.2
  13.1 7.3 %all-to-all-start.2 = ((bf16[32,2,128]{2,1,0:T(2,128)(2,1)}), bf16[32,2,128]{2,1,0:T(2,128)(2,1)S(1)}, u32[]{:S(2)}, u32[]{:S(2)}) async-start(bf16[32,2,128]{2,1,0:T(2,128)(2,1)} %reshape.345), calls=%async_computation.2 | async-start | bytes 32768 | tf_op jit(solution)/shard_map/all_to_all | solution.py:97
  22.0 2.7 gather_fusion.1
  24.7 1.9 gather_fusion
  27.5 4.9 %all-to-all-start.1 = ((bf16[32,8,128]{2,1,0:T(8,128)(2,1)}), bf16[32,8,128]{2,1,0:T(8,128)(2,1)S(1)}, u32[]{:S(2)}, u32[]{:S(2)}) async-start(bf16[32,8,128]{2,1,0:T(8,128)(2,1)} %bitcast.9), calls=%async_computation.1 | async-start | bytes 131072 | tf_op jit(solution)/shard_map/all_to_all | solution.py:90
  33.0 6.7 %all-to-all-done.1 = bf16[32,8,128]{2,1,0:T(8,128)(2,1)S(1)} async-done(((bf16[32,8,128]{2,1,0:T(8,128)(2,1)}), bf16[32,8,128]{2,1,0:T(8,128)(2,1)S(1)}, u32[]{:S(2)}, u32[]{:S(2)}) %all-to-all-start.1) | async-done | bytes 65568 | tf_op jit(solution)/shard_map/all_to_all | solution.py:90
  39.7 2.6 all-to-all-start
  42.9 5.2 %all-gather.3 = s32[4,1,512]{2,1,0:T(1,128)S(1)} all-gather(s32[1,1,512]{2,1,0:T(1,128)S(1)} %bitcast.126), channel_id=1, replica_groups=mesh['group'=4,'rep'=8] {'group'}, dimensions={0}, use_global_device_ids=true | all-gather | bytes 10240 | tf_op jit(solution)/shard_map/all_gather | solution.py:122
  48.6 4.1 %all-to-all-done = bf16[32,8,512]{2,1,0:T(8,128)(2,1)S(1)} async-done(((bf16[32,8,512]{2,1,0:T(8,128)(2,1)}), bf16[32,8,512]{2,1,0:T(8,128)(2,1)S(1)}, u32[]{:S(2)}, u32[]{:S(2)}) %all-to-all-start) | async-done | bytes 262176 | tf_op jit(solution)/shard_map/all_to_all | solution.py:89
  53.4 16.6 %gather_fusion.3 = bf16[4096,256]{1,0:T(8,128)(2,1)S(1)} fusion(bf16[768,256]{1,0:T(8,128)(2,1)S(1)} %pad_maximum_fusion, s32[4096]{0:T(1024)} %bitcast_clamp_fusion), kind=kCustom, calls=%fused_computation.3 | custom fusion | bytes 4210688 | tf_op jit(solution)/shard_map/gather | solution.py:113
  70.0 1.2 reduce_sum.61
  71.2 1.2 copy.33
  72.5 4.5 %multiply_convert_fusion.1 = (bf16[1024,1024]{1,0:T(8,128)(2,1)S(1)}, f32[1024,1024]{1,0:T(8,128)}) fusion(bf16[1024,256]{1,0:T(8,128)(2,1)} %reduce_sum.61, bf16[256,1024]{1,0:T(8,128)(2,1)} %param.21), kind=kOutput, calls=%fused_computation.24 | convolution fusion | flops 542113792 | bytes 7340032 | tf_op jit(solution)/shard_map/dot_general | solution.py:114
  77.0 1.3 copy-done.2
  79.2 2.5 multiply_reduce_fusion
  81.7 5.2 %all-gather = f32[8192]{0:T(1024)S(1)} all-gather(f32[2048]{0:T(1024)S(1)} %get-tuple-element.88), channel_id=2, replica_groups=mesh['group'=4,'rep'=8] {'group'}, dimensions={0}, use_global_device_ids=true | all-gather | bytes 40960 | tf_op jit(solution)/shard_map/all_gather | solution.py:11
  86.9 2.7 fusion
  89.6 5.2 %all-gather.1 = f32[8192]{0:T(1024)S(1)} all-gather(f32[2048]{0:T(1024)S(1)} %get-tuple-element.53), channel_id=3, replica_groups=mesh['group'=4,'rep'=8] {'group'}, dimensions={0}, use_global_device_ids=true | all-gather | bytes 40960 | tf_op jit(solution)/shard_map/all_gather | solution.py:11
  94.8 5.4 %all-gather.2 = f32[8192]{0:T(1024)S(1)} all-gather(f32[2048]{0:T(1024)S(1)} %get-tuple-element.52), channel_id=4, replica_groups=mesh['group'=4,'rep'=8] {'group'}, dimensions={0}, use_global_device_ids=true | all-gather | bytes 40960 | tf_op jit(solution)/shard_map/all_gather | solution.py:11
  100.6 4.8 %fusion.2 = bf16[2048,1024]{0,1:T(8,128)(2,1)S(1)} fusion(f32[1024,2048]{1,0:T(8,128)} %copy-done.1, f32[2048]{0:T(1024)S(1)} %log_add_fusion, s32[2048]{0:T(1024)} %bitcast.117, s32[1024]{0:T(1024)S(1)} %iota_add_fusion), kind=kLoop, calls=%fused_computation.16 | loop fusion | flops 12582912 | bytes 12603392 | tf_op jit(solution)/shard_map/convert_element_type | solution.py:139
  105.4 1.3 multiply_reduce_fusion.1
  107.8 1.3 copy-done.27
  109.1 1.9 multiply_convert_fusion
  112.1 1.8 fusion.43
  113.9 1.7 fusion.44
  115.6 1.3 copy.35
  117.0 3.5 %broadcast_in_dim.27 = f32[4,1024,256]{2,1,0:T(8,128)} broadcast(f32[1024,256]{1,0:T(8,128)} %copy.35), dimensions={1,2} | broadcast | bytes 5242880 | tf_op jit(solution)/shard_map/broadcast_in_dim | solution.py:160
  120.5 23.0 %scatter_custom_fusion = f32[768,256]{1,0:T(8,128)S(1)} fusion(s32[4096]{0:T(1024)} %bitcast.118, f32[4096,256]{1,0:T(8,128)} %bitcast.110, f32[]{:T(128)} %constant.85.clone.1), kind=kCustom, calls=%fused_computation.52 | custom fusion | flops 1048576 | bytes 786944 | tf_op jit(solution)/shard_map/scatter-add | solution.py:163
  143.6 1.1 fusion.22
  144.7 1.7 fusion.30
  146.5 4.6 %fusion.6 = bf16[2048,256]{1,0:T(8,128)(2,1)} fusion(bf16[2048,1024]{0,1:T(8,128)(2,1)} %copy-done.5, f32[1024,256]{0,1:T(8,128)S(1)} %get-tuple-element.87, f32[1024]{0:T(1024)S(1)} %get-tuple-element.78), kind=kOutput, calls=%fused_computation.27 | convolution fusion | flops 1075314688 | bytes 6295552 | tf_op jit(solution)/shard_map/dot_general | solution.py:144
  152.2 2.8 all-to-all-start.5
  155.8 6.2 %all-to-all-done.5 = bf16[32,2,128]{2,1,0:T(2,128)(2,1)S(1)} async-done(((bf16[32,2,128]{2,1,0:T(2,128)(2,1)}), bf16[32,2,128]{2,1,0:T(2,128)(2,1)S(1)}, u32[]{:S(2)}, u32[]{:S(2)}) %all-to-all-start.5) | async-done | bytes 16416 | tf_op jit(solution)/shard_map/all_to_all | solution.py:189
  162.0 2.6 all-to-all-start.4
  165.6 6.7 %all-to-all-done.4 = bf16[32,8,128]{2,1,0:T(8,128)(2,1)S(1)} async-done(((bf16[32,8,128]{2,1,0:T(8,128)(2,1)}), bf16[32,8,128]{2,1,0:T(8,128)(2,1)S(1)}, u32[]{:S(2)}, u32[]{:S(2)}) %all-to-all-start.4) | async-done | bytes 65568 | tf_op jit(solution)/shard_map/all_to_all | solution.py:180
  172.3 2.6 all-to-all-start.3
  175.1 40.9 %psum.37 = f32[32,256]{1,0:T(8,128)S(1)} all-reduce(f32[32,256]{1,0:T(8,128)S(1)} %fusion.27), channel_id=1, replica_groups=mesh['group'=4,'rep'=8] {'group','rep'}, use_global_device_ids=true, to_apply=%region_16.17 | all-reduce | flops 8192 | bytes 65536 | tf_op jit(solution)/shard_map/psum | solution.py:211
  216.0 1.3 dynamic-slice_subtract_fusion
  218.3 3.0 scatter_custom_fusion.3
  221.3 3.0 scatter_custom_fusion.2
  224.2 3.7 %scatter_custom_fusion.1 = f32[1024,512]{1,0:T(8,128)} fusion(s32[256]{0:T(256)} %bitcast.120, f32[]{:T(128)} %constant.85.clone.1, bf16[32,8,512]{2,1,0:T(8,128)(2,1)S(1)} %all-to-all-done.3), kind=kCustom, calls=%fused_computation.46 | custom fusion | flops 262144 | bytes 2359808 | tf_op jit(solution)/shard_map/scatter-add | solution.py:202
  227.9 55.4 %all-reduce.3.cloned.1.call-done = (f32[512,256]{0,1:T(8,128)}, f32[128,256]{0,1:T(8,128)}, f32[256,1024]{1,0:T(8,128)}, f32[1024,256]{0,1:T(8,128)}) async-done(((f32[512,256]{0,1:T(8,128)}, f32[128,256]{0,1:T(8,128)}, f32[256,1024]{1,0:T(8,128)}, f32[1024,256]{0,1:T(8,128)}), (f32[512,256]{0,1:T(8,128)}, f32[128,256]{0,1:T(8,128)}, f32[256,1024]{1,0:T(8,128)}, ...) | async-done | bytes 2752528 | tf_op jit(solution)/shard_map/psum | solution.py:211
  283.3 1.3 constant_dynamic-slice_fusion.6
  284.6 1.5 constant_dynamic-slice_fusion.7
  286.1 1.6 constant_dynamic-slice_fusion.3
  287.7 1.6 constant_dynamic-slice_fusion.4
  289.2 20.4 %reduce-scatter.2.cloned.1.call-done = bf16[512,256]{1,0:T(8,128)(2,1)} async-done(((bf16[2048,256]{1,0:T(8,128)(2,1)}), bf16[512,256]{1,0:T(8,128)(2,1)}) %reduce-scatter.2.cloned.1.call-update) | async-done | bytes 262160 | tf_op jit(solution)/shard_map/reduce_scatter | solution.py:143
  309.6 1.8 convert_element_type.86
  (123 shorter events, 16.1 us)
Async XLA Ops:
  7.2 17.5 %copy-start = (bf16[1024,512]{1,0:T(8,128)(2,1)S(1)}, bf16[1024,512]{1,0:T(8,128)(2,1)}, u32[]{:S(2)}) copy-start(bf16[1024,512]{1,0:T(8,128)(2,1)} %param.15) | copy-start | bytes 3145732
  7.2 35.7 %copy-start.26 = (s32[512]{0:T(512)S(1)}, s32[512]{0:T(512)}, u32[]{:S(2)}) copy-start(s32[512]{0:T(512)} %param.24) | copy-start | bytes 6148
  7.2 41.0 %copy-start.20 = (bf16[32,256]{1,0:T(8,128)(2,1)S(1)}, bf16[32,256]{1,0:T(8,128)(2,1)}, u32[]{:S(2)}) copy-start(bf16[32,256]{1,0:T(8,128)(2,1)} %param.20) | copy-start | bytes 49156
  7.2 41.2 %copy-start.16 = (bf16[128,256]{1,0:T(8,128)(2,1)S(1)}, bf16[128,256]{1,0:T(8,128)(2,1)}, u32[]{:S(2)}) copy-start(bf16[128,256]{1,0:T(8,128)(2,1)} %param.19) | copy-start | bytes 196612
  7.2 45.5 %copy-start.9 = (bf16[512,256]{1,0:T(8,128)(2,1)S(1)}, bf16[512,256]{1,0:T(8,128)(2,1)}, u32[]{:S(2)}) copy-start(bf16[512,256]{1,0:T(8,128)(2,1)} %param.18) | copy-start | bytes 786436
  7.2 71.9 %all-gather.6.cloned.1.call-start = ((), (), s32[]{:S(2)}) async-start(), calls=%async_computation.7 | async-start | bytes 1310720 | tf_op jit(solution)/shard_map/all_gather | solution.py:121
  8.7 4.4 %copy-start.25 = (s32[256,1]{0,1:T(1,128)}, s32[256,1]{0,1:T(1,128)S(1)}, u32[]{:S(2)}) copy-start(s32[256,1]{0,1:T(1,128)S(1)} %get-tuple-element.80) | copy-start | bytes 3076
  8.7 13.2 %copy-start.24 = (s32[256,1]{0,1:T(1,128)}, s32[256,1]{0,1:T(1,128)S(1)}, u32[]{:S(2)}) copy-start(s32[256,1]{0,1:T(1,128)S(1)} %get-tuple-element.81) | copy-start | bytes 3076
  8.7 34.2 %copy-start.23 = (s32[256,1]{0,1:T(1,128)}, s32[256,1]{0,1:T(1,128)S(1)}, u32[]{:S(2)}) copy-start(s32[256,1]{0,1:T(1,128)S(1)} %get-tuple-element.79) | copy-start | bytes 3076
  13.1 14.4 %all-to-all-start.2 = ((bf16[32,2,128]{2,1,0:T(2,128)(2,1)}), bf16[32,2,128]{2,1,0:T(2,128)(2,1)S(1)}, u32[]{:S(2)}, u32[]{:S(2)}) async-start(bf16[32,2,128]{2,1,0:T(2,128)(2,1)} %reshape.345), calls=%async_computation.2 | async-start | bytes 32768 | tf_op jit(solution)/shard_map/all_to_all | solution.py:97
  27.5 12.2 %all-to-all-start.1 = ((bf16[32,8,128]{2,1,0:T(8,128)(2,1)}), bf16[32,8,128]{2,1,0:T(8,128)(2,1)S(1)}, u32[]{:S(2)}, u32[]{:S(2)}) async-start(bf16[32,8,128]{2,1,0:T(8,128)(2,1)} %bitcast.9), calls=%async_computation.1 | async-start | bytes 131072 | tf_op jit(solution)/shard_map/all_to_all | solution.py:90
  39.7 13.3 %copy-start.13 = (bf16[32,8,128]{2,1,0:T(8,128)(2,1)}, bf16[32,8,128]{2,1,0:T(8,128)(2,1)S(1)}, u32[]{:S(2)}) copy-start(bf16[32,8,128]{2,1,0:T(8,128)(2,1)S(1)} %all-to-all-done.1) | copy-start | bytes 196612
  39.7 13.0 %all-to-all-start = ((bf16[32,8,512]{2,1,0:T(8,128)(2,1)}), bf16[32,8,512]{2,1,0:T(8,128)(2,1)S(1)}, u32[]{:S(2)}, u32[]{:S(2)}) async-start(bf16[32,8,512]{2,1,0:T(8,128)(2,1)} %bitcast.5), calls=%async_computation | async-start | bytes 524288 | tf_op jit(solution)/shard_map/all_to_all | solution.py:89
  42.3 241.1 %all-reduce.3.cloned.1.call-start = ((), (), s32[]{:S(2)}) async-start(), calls=%async_computation.9 | async-start | bytes 5505024 | tf_op jit(solution)/shard_map/psum | solution.py:211
  48.1 38.8 %copy-start.18 = (s32[4,1,512]{2,1,0:T(1,128)}, s32[4,1,512]{2,1,0:T(1,128)S(1)}, u32[]{:S(2)}) copy-start(s32[4,1,512]{2,1,0:T(1,128)S(1)} %all-gather.3) | copy-start | bytes 24580
  48.2 4.7 %copy-start.11 = (bf16[256,32]{1,0:T(8,128)(2,1)}, bf16[256,32]{1,0:T(8,128)(2,1)S(1)}, u32[]{:S(2)}) copy-start(bf16[256,32]{1,0:T(8,128)(2,1)S(1)} %reshape.346) | copy-start | bytes 49156
  52.7 0.7 copy-start.6
  72.5 5.9 %copy-start.14 = (bf16[1024,256]{1,0:T(8,128)(2,1)S(1)}, bf16[1024,256]{1,0:T(8,128)(2,1)}, u32[]{:S(2)}) copy-start(bf16[1024,256]{1,0:T(8,128)(2,1)} %param.22) | copy-start | bytes 1572868
  77.0 1.3 copy-start.2
  81.7 7.9 %copy-start.1 = (f32[1024,2048]{1,0:T(8,128)}, f32[1024,2048]{1,0:T(8,128)S(1)}, u32[]{:S(2)}) copy-start(f32[1024,2048]{1,0:T(8,128)S(1)} %get-tuple-element.89) | copy-start | bytes 25165828
  100.6 4.8 %copy-start.19 = (f32[2048]{0:T(1024)}, f32[2048]{0:T(1024)S(1)}, u32[]{:S(2)}) copy-start(f32[2048]{0:T(1024)S(1)} %log_add_fusion) | copy-start | bytes 24580
  100.6 4.8 %copy-start.8 = (bf16[2048,256]{1,0:T(8,128)(2,1)S(1)}, bf16[2048,256]{1,0:T(8,128)(2,1)}, u32[]{:S(2)}) copy-start(bf16[2048,256]{1,0:T(8,128)(2,1)} %all-gather.6.cloned.1.call-done) | copy-start | bytes 3145732
  105.4 2.1 copy-start.5
  105.4 3.7 %copy-start.27 = (f32[1024,1024]{1,0:T(8,128)S(1)}, f32[1024,1024]{1,0:T(8,128)}, u32[]{:S(2)}) copy-start(f32[1024,1024]{1,0:T(8,128)} %get-tuple-element.85) | copy-start | bytes 12582916
  109.1 1.9 copy-start.15
  111.0 1.0 copy-start.4
  111.1 2.8 copy-start.3
  115.6 27.9 %copy-start.7 = (bf16[32,8,512]{2,1,0:T(8,128)(2,1)S(1)}, bf16[32,8,512]{2,1,0:T(8,128)(2,1)}, u32[]{:S(2)}) copy-start(bf16[32,8,512]{2,1,0:T(8,128)(2,1)} %copy-done.6) | copy-start | bytes 786436
  146.4 4.7 %copy-start.21 = (bf16[32,256]{1,0:T(8,128)(2,1)S(1)}, bf16[32,256]{1,0:T(8,128)(2,1)}, u32[]{:S(2)}) copy-start(bf16[32,256]{1,0:T(8,128)(2,1)} %param.20) | copy-start | bytes 49156
  146.4 8.5 %copy-start.17 = (bf16[128,256]{1,0:T(8,128)(2,1)S(1)}, bf16[128,256]{1,0:T(8,128)(2,1)}, u32[]{:S(2)}) copy-start(bf16[128,256]{1,0:T(8,128)(2,1)} %param.19) | copy-start | bytes 196612
  146.4 18.2 %copy-start.10 = (bf16[512,256]{1,0:T(8,128)(2,1)S(1)}, bf16[512,256]{1,0:T(8,128)(2,1)}, u32[]{:S(2)}) copy-start(bf16[512,256]{1,0:T(8,128)(2,1)} %param.18) | copy-start | bytes 786436
  146.4 28.5 %copy-start.12 = (bf16[256,32]{1,0:T(8,128)(2,1)S(1)}, bf16[256,32]{1,0:T(8,128)(2,1)}, u32[]{:S(2)}) copy-start(bf16[256,32]{1,0:T(8,128)(2,1)} %copy-done.11) | copy-start | bytes 49156
  146.5 71.7 %copy-start.22 = (f32[256,4]{0,1:T(4,128)S(1)}, f32[256,4]{0,1:T(4,128)}, u32[]{:S(2)}) copy-start(f32[256,4]{0,1:T(4,128)} %get-tuple-element.82) | copy-start | bytes 12292
  146.5 163.1 %reduce-scatter.2.cloned.1.call-start = ((), (), s32[]{:S(2)}) async-start(), calls=%async_computation.8 | async-start | bytes 1310720 | tf_op jit(solution)/shard_map/reduce_scatter | solution.py:143
  152.2 9.8 %all-to-all-start.5 = ((bf16[32,2,128]{2,1,0:T(2,128)(2,1)}), bf16[32,2,128]{2,1,0:T(2,128)(2,1)S(1)}, u32[]{:S(2)}, u32[]{:S(2)}) async-start(bf16[32,2,128]{2,1,0:T(2,128)(2,1)} %convert_element_type.98), calls=%async_computation.6 | async-start | bytes 32768 | tf_op jit(solution)/shard_map/all_to_all | solution.py:189
  162.0 10.3 %all-to-all-start.4 = ((bf16[32,8,128]{2,1,0:T(8,128)(2,1)}), bf16[32,8,128]{2,1,0:T(8,128)(2,1)S(1)}, u32[]{:S(2)}, u32[]{:S(2)}) async-start(bf16[32,8,128]{2,1,0:T(8,128)(2,1)} %fusion.10), calls=%async_computation.5 | async-start | bytes 131072 | tf_op jit(solution)/shard_map/all_to_all | solution.py:180
  172.3 51.9 %all-to-all-start.3 = ((bf16[32,8,512]{2,1,0:T(8,128)(2,1)}), bf16[32,8,512]{2,1,0:T(8,128)(2,1)S(1)}, u32[]{:S(2)}, u32[]{:S(2)}) async-start(bf16[32,8,512]{2,1,0:T(8,128)(2,1)} %fusion.9), calls=%async_computation.4 | async-start | bytes 524288 | tf_op jit(solution)/shard_map/all_to_all | solution.py:171
Sparse Core Ops, SparseCore 0:
  9.6 19.5 all-gather.5
  146.5 136.7 all-reduce.2
  285.8 23.7 reduce-scatter.1
where the time goes:
time: 319 us; the launch traced here: 318 us
  waiting for transfers between devices  101 us (32%)
  blocking collectives  61.8 us (19%)
  other arithmetic  48.3 us (15%)
  local copies, waits for them, and re-layouts  43.6 us (14%)
  matrix products  25.5 us (8%)
  starting transfers between devices  22.8 us (7%)
  between operations  14.4 us (5%)
    psum x1, waiting for transfers between devices, local(): lax.psum((grad_ph, grad_pm, grad_pc, grad_in_local, grad_out_local), ('gr...  55.4 us
    psum x1, blocking collectives, local(): lax.psum((grad_ph, grad_pm, grad_pc, grad_in_local, grad_out_local), ('gr...  40.9 us
    scatter-add x1, other arithmetic, local(): jax.ops.segment_sum(stacked, slot_index.reshape(-1), num_segments=3 * slo...  23 us
    reduce_scatter x1, waiting for transfers between devices, local(): lax.psum_scatter((LOGIT_SCALE * jnp.dot(score_grad, vectors, preferred_el...  20.4 us
    gather x1, local copies, waits for them, and re-layouts, local(): slot_table[slot_index].astype(jnp.float32)  16.6 us
    all_gather x3, blocking collectives, merged(): pieces = jax.tree.map(lambda part: lax.all_gather(part, axis), value)  15.7 us
    dot_general x6, matrix products, contract(): lax.dot_general(left_rows, right_rows, (((0,), (0,)), ((), ())), preferre...  7.8 us
    all_to_all x1, starting transfers between devices, local(): lax.all_to_all(rows_cold.reshape(devices, slots_each // 4, 4 * cold_width...  7.33 us
  transfers between devices with their start and end apart: 9, of which 7 were waited for; matrix products, arithmetic and copies ran while one was open for 20% of the time, Pallas kernels for 0%

commit v1 on v0

--- a/solution.py
+++ b/solution.py
@@ -208,7 +208,9 @@
     grad_cold = cold_add(served[2], back_cold.reshape(slot_total, cold_width), table_cold.shape)
     grad_in_local = contract(pooled, pre_grad)
     grad_out_local = contract(hidden, wide_low)
-    totals = lax.psum((grad_ph, grad_pm, grad_pc, grad_in_local, grad_out_local), ("group", "rep"))
+    totals = lax.psum(
+        lax.psum((grad_ph, grad_pm, grad_pc, grad_in_local, grad_out_local), "rep"), "group"
+    )
     rep_count = lax.axis_size("rep")
     rep_at = lax.axis_index("rep")
     summed = tuple(

time: 319 us -> 368 us (1.15)
  waiting for transfers between devices: 101 us -> 142 us
  blocking collectives: 61.8 us -> 69.5 us
    psum x1 -> x2, waiting for transfers between devices: 55.4 us -> 117 us  [the longest x1 112 us: local(): lax.psum((grad_ph, grad_pm, grad_pc, grad_in_local, grad_out_local), 'rep')]
    reduce_scatter x1, waiting for transfers between devices: 20.4 us -> 0.01 us  [local(): lax.psum_scatter((LOGIT_SCALE * jnp.dot(score_grad, vectors, preferred_el...]
    psum x1 -> x2, blocking collectives: 40.9 us -> 48.6 us  [the longest x1 37.4 us: local(): lax.psum((grad_ph, grad_pm, grad_pc, grad_in_local, grad_out_local), 'rep')]
  transfers between devices with their start and end apart: 9 -> 10, of which waited for: 7 -> 7; matrix products, arithmetic and copies ran while one was open for 20% -> 16% of each run, Pallas kernels for 0% -> 0%
where the time goes in v1:
time: 368 us; the launch traced here: 367 us
  waiting for transfers between devices  142 us (39%)
  blocking collectives  69.5 us (19%)
  other arithmetic  48.3 us (13%)
  local copies, waits for them, and re-layouts  43.6 us (12%)
  matrix products  25.2 us (7%)
  starting transfers between devices  23.7 us (6%)
  between operations  14.4 us (4%)
    psum x1, waiting for transfers between devices, local(): lax.psum((grad_ph, grad_pm, grad_pc, grad_in_local, grad_out_local), 'rep')  112 us
    psum x1, blocking collectives, local(): lax.psum((grad_ph, grad_pm, grad_pc, grad_in_local, grad_out_local), 'rep')  37.4 us
    scatter-add x1, other arithmetic, local(): jax.ops.segment_sum(stacked, slot_index.reshape(-1), num_segments=3 * slo...  23 us
    gather x1, local copies, waits for them, and re-layouts, local(): slot_table[slot_index].astype(jnp.float32)  16.6 us
    all_gather x3, blocking collectives, merged(): pieces = jax.tree.map(lambda part: lax.all_gather(part, axis), value)  15.7 us
    psum x1, blocking collectives, local(): lax.psum(lax.psum((grad_ph, grad_pm, grad_pc, grad_in_local, grad_out_loc...  11.2 us
    dot_general x6, matrix products, contract(): lax.dot_general(left_rows, right_rows, (((0,), (0,)), ((), ())), preferre...  7.66 us
  transfers between devices with their start and end apart: 10, of which 7 were waited for; matrix products, arithmetic and copies ran while one was open for 16% of the time, Pallas kernels for 0%

profile of v1, /device:TPU:0, one launch (start us, length us, event | category | flops | bytes accessed | tf_op | source)
XLA Modules:
  0.0 367.0 jit_solution(16189390172835464637)
XLA Ops:
  9.4 2.1 gather_fusion.2
  13.1 7.3 %all-to-all-start.2 = ((bf16[32,2,128]{2,1,0:T(2,128)(2,1)}), bf16[32,2,128]{2,1,0:T(2,128)(2,1)S(1)}, u32[]{:S(2)}, u32[]{:S(2)}) async-start(bf16[32,2,128]{2,1,0:T(2,128)(2,1)} %reshape.345), calls=%async_computation.2 | async-start | bytes 32768 | tf_op jit(solution)/shard_map/all_to_all | solution.py:97
  22.0 2.7 gather_fusion.1
  24.7 1.9 gather_fusion
  27.5 4.9 %all-to-all-start.1 = ((bf16[32,8,128]{2,1,0:T(8,128)(2,1)}), bf16[32,8,128]{2,1,0:T(8,128)(2,1)S(1)}, u32[]{:S(2)}, u32[]{:S(2)}) async-start(bf16[32,8,128]{2,1,0:T(8,128)(2,1)} %bitcast.9), calls=%async_computation.1 | async-start | bytes 131072 | tf_op jit(solution)/shard_map/all_to_all | solution.py:90
  33.0 6.7 %all-to-all-done.1 = bf16[32,8,128]{2,1,0:T(8,128)(2,1)S(1)} async-done(((bf16[32,8,128]{2,1,0:T(8,128)(2,1)}), bf16[32,8,128]{2,1,0:T(8,128)(2,1)S(1)}, u32[]{:S(2)}, u32[]{:S(2)}) %all-to-all-start.1) | async-done | bytes 65568 | tf_op jit(solution)/shard_map/all_to_all | solution.py:90
  39.7 2.6 all-to-all-start
  42.9 5.2 %all-gather.3 = s32[4,1,512]{2,1,0:T(1,128)S(1)} all-gather(s32[1,1,512]{2,1,0:T(1,128)S(1)} %bitcast.126), channel_id=1, replica_groups=mesh['group'=4,'rep'=8] {'group'}, dimensions={0}, use_global_device_ids=true | all-gather | bytes 10240 | tf_op jit(solution)/shard_map/all_gather | solution.py:122
  48.6 4.1 %all-to-all-done = bf16[32,8,512]{2,1,0:T(8,128)(2,1)S(1)} async-done(((bf16[32,8,512]{2,1,0:T(8,128)(2,1)}), bf16[32,8,512]{2,1,0:T(8,128)(2,1)S(1)}, u32[]{:S(2)}, u32[]{:S(2)}) %all-to-all-start) | async-done | bytes 262176 | tf_op jit(solution)/shard_map/all_to_all | solution.py:89
  53.4 16.6 %gather_fusion.3 = bf16[4096,256]{1,0:T(8,128)(2,1)S(1)} fusion(bf16[768,256]{1,0:T(8,128)(2,1)S(1)} %pad_maximum_fusion, s32[4096]{0:T(1024)} %bitcast_clamp_fusion), kind=kCustom, calls=%fused_computation.3 | custom fusion | bytes 4210688 | tf_op jit(solution)/shard_map/gather | solution.py:113
  70.0 1.2 reduce_sum.61
  71.2 1.2 copy.33
  72.5 4.5 %multiply_convert_fusion.1 = (bf16[1024,1024]{1,0:T(8,128)(2,1)S(1)}, f32[1024,1024]{1,0:T(8,128)}) fusion(bf16[1024,256]{1,0:T(8,128)(2,1)} %reduce_sum.61, bf16[256,1024]{1,0:T(8,128)(2,1)} %param.21), kind=kOutput, calls=%fused_computation.24 | convolution fusion | flops 542113792 | bytes 7340032 | tf_op jit(solution)/shard_map/dot_general | solution.py:114
  76.9 1.3 copy-done.2
  79.1 2.5 multiply_reduce_fusion
  81.6 5.2 %all-gather = f32[8192]{0:T(1024)S(1)} all-gather(f32[2048]{0:T(1024)S(1)} %get-tuple-element.92), channel_id=2, replica_groups=mesh['group'=4,'rep'=8] {'group'}, dimensions={0}, use_global_device_ids=true | all-gather | bytes 40960 | tf_op jit(solution)/shard_map/all_gather | solution.py:11
  86.8 2.7 fusion
  89.5 5.2 %all-gather.1 = f32[8192]{0:T(1024)S(1)} all-gather(f32[2048]{0:T(1024)S(1)} %get-tuple-element.53), channel_id=3, replica_groups=mesh['group'=4,'rep'=8] {'group'}, dimensions={0}, use_global_device_ids=true | all-gather | bytes 40960 | tf_op jit(solution)/shard_map/all_gather | solution.py:11
  94.7 5.4 %all-gather.2 = f32[8192]{0:T(1024)S(1)} all-gather(f32[2048]{0:T(1024)S(1)} %get-tuple-element.52), channel_id=4, replica_groups=mesh['group'=4,'rep'=8] {'group'}, dimensions={0}, use_global_device_ids=true | all-gather | bytes 40960 | tf_op jit(solution)/shard_map/all_gather | solution.py:11
  100.5 4.8 %fusion.2 = bf16[2048,1024]{0,1:T(8,128)(2,1)S(1)} fusion(f32[1024,2048]{1,0:T(8,128)} %copy-done.1, f32[2048]{0:T(1024)S(1)} %log_add_fusion, s32[2048]{0:T(1024)} %bitcast.117, s32[1024]{0:T(1024)S(1)} %iota_add_fusion), kind=kLoop, calls=%fused_computation.16 | loop fusion | flops 12582912 | bytes 12603392 | tf_op jit(solution)/shard_map/convert_element_type | solution.py:139
  105.3 1.3 multiply_reduce_fusion.1
  107.7 1.3 copy-done.27
  109.0 1.9 multiply_convert_fusion
  112.0 1.7 fusion.43
  113.7 1.7 fusion.44
  115.4 1.3 copy.35
  116.7 3.5 broadcast_in_dim.27
  120.3 23.0 %scatter_custom_fusion = f32[768,256]{1,0:T(8,128)S(1)} fusion(s32[4096]{0:T(1024)} %bitcast.118, f32[4096,256]{1,0:T(8,128)} %bitcast.110, f32[]{:T(128)} %constant.85.clone.1), kind=kCustom, calls=%fused_computation.52 | custom fusion | flops 1048576 | bytes 786944 | tf_op jit(solution)/shard_map/scatter-add | solution.py:163
  144.4 1.7 fusion.30
  146.2 4.5 %fusion.6 = bf16[2048,256]{1,0:T(8,128)(2,1)} fusion(bf16[2048,1024]{0,1:T(8,128)(2,1)} %copy-done.5, f32[1024,256]{0,1:T(8,128)S(1)} %get-tuple-element.91, f32[1024]{0:T(1024)S(1)} %get-tuple-element.82), kind=kOutput, calls=%fused_computation.27 | convolution fusion | flops 1075314688 | bytes 6295552 | tf_op jit(solution)/shard_map/dot_general | solution.py:144
  150.9 112.4 %all-reduce.5.cloned.1.call-done = (f32[512,256]{0,1:T(8,128)}, f32[128,256]{0,1:T(8,128)}, f32[256,1024]{1,0:T(8,128)}, f32[1024,256]{0,1:T(8,128)}) async-done(((f32[512,256]{0,1:T(8,128)}, f32[128,256]{0,1:T(8,128)}, f32[256,1024]{1,0:T(8,128)}, f32[1024,256]{0,1:T(8,128)}), (f32[512,256]{0,1:T(8,128)}, f32[128,256]{0,1:T(8,128)}, f32[256,1024]{1,0:T(8,128)}, ...) | async-done | bytes 2752528 | tf_op jit(solution)/shard_map/psum | solution.py:212
  264.4 3.6 all-to-all-start.5
  268.8 6.2 %all-to-all-done.5 = bf16[32,2,128]{2,1,0:T(2,128)(2,1)S(1)} async-done(((bf16[32,2,128]{2,1,0:T(2,128)(2,1)}), bf16[32,2,128]{2,1,0:T(2,128)(2,1)S(1)}, u32[]{:S(2)}, u32[]{:S(2)}) %all-to-all-start.5) | async-done | bytes 16416 | tf_op jit(solution)/shard_map/all_to_all | solution.py:189
  275.0 2.6 all-to-all-start.4
  278.6 6.4 %all-to-all-done.4 = bf16[32,8,128]{2,1,0:T(8,128)(2,1)S(1)} async-done(((bf16[32,8,128]{2,1,0:T(8,128)(2,1)}), bf16[32,8,128]{2,1,0:T(8,128)(2,1)S(1)}, u32[]{:S(2)}, u32[]{:S(2)}) %all-to-all-start.4) | async-done | bytes 65568 | tf_op jit(solution)/shard_map/all_to_all | solution.py:180
  285.0 2.6 all-to-all-start.3
  287.8 37.4 %psum.74 = f32[32,256]{1,0:T(8,128)S(1)} all-reduce(f32[32,256]{1,0:T(8,128)S(1)} %fusion.27), channel_id=1, replica_groups=mesh['group'=4,'rep'=8] {'rep'}, use_global_device_ids=true, to_apply=%region_18.19 | all-reduce | flops 8192 | bytes 65536 | tf_op jit(solution)/shard_map/psum | solution.py:212
  325.1 11.2 %psum.75 = f32[32,256]{1,0:T(8,128)S(1)} all-reduce(f32[32,256]{1,0:T(8,128)S(1)} %psum.74), channel_id=1, replica_groups=mesh['group'=4,'rep'=8] {'group'}, use_global_device_ids=true, to_apply=%region_19.20 | all-reduce | flops 8192 | bytes 65536 | tf_op jit(solution)/shard_map/psum | solution.py:211
  336.3 1.3 dynamic-slice_subtract_fusion
  338.6 3.0 scatter_custom_fusion.3
  341.6 3.0 scatter_custom_fusion.2
  344.6 3.7 scatter_custom_fusion.1
  348.2 1.8 convert_element_type.86
  350.0 4.5 %all-reduce.7.cloned.1.call-done = (f32[512,256]{0,1:T(8,128)}, f32[128,256]{0,1:T(8,128)}, f32[256,1024]{1,0:T(8,128)}, f32[1024,256]{0,1:T(8,128)}) async-done(((f32[512,256]{0,1:T(8,128)}, f32[128,256]{0,1:T(8,128)}, f32[256,1024]{1,0:T(8,128)}, f32[1024,256]{0,1:T(8,128)}), (f32[512,256]{0,1:T(8,128)}, f32[128,256]{0,1:T(8,128)}, f32[256,1024]{1,0:T(8,128)}, ...) | async-done | bytes 2752528 | tf_op jit(solution)/shard_map/psum | solution.py:211
  354.5 1.5 constant_dynamic-slice_fusion.7
  356.0 1.3 constant_dynamic-slice_fusion.6
  357.3 1.6 constant_dynamic-slice_fusion.3
  358.9 1.6 constant_dynamic-slice_fusion.4
  (127 shorter events, 17.2 us)
Async XLA Ops:
  7.2 17.5 %copy-start = (bf16[1024,512]{1,0:T(8,128)(2,1)S(1)}, bf16[1024,512]{1,0:T(8,128)(2,1)}, u32[]{:S(2)}) copy-start(bf16[1024,512]{1,0:T(8,128)(2,1)} %param.15) | copy-start | bytes 3145732
  7.2 35.7 %copy-start.26 = (s32[512]{0:T(512)S(1)}, s32[512]{0:T(512)}, u32[]{:S(2)}) copy-start(s32[512]{0:T(512)} %param.24) | copy-start | bytes 6148
  7.2 41.0 %copy-start.20 = (bf16[32,256]{1,0:T(8,128)(2,1)S(1)}, bf16[32,256]{1,0:T(8,128)(2,1)}, u32[]{:S(2)}) copy-start(bf16[32,256]{1,0:T(8,128)(2,1)} %param.20) | copy-start | bytes 49156
  7.2 41.2 %copy-start.16 = (bf16[128,256]{1,0:T(8,128)(2,1)S(1)}, bf16[128,256]{1,0:T(8,128)(2,1)}, u32[]{:S(2)}) copy-start(bf16[128,256]{1,0:T(8,128)(2,1)} %param.19) | copy-start | bytes 196612
  7.2 45.5 %copy-start.9 = (bf16[512,256]{1,0:T(8,128)(2,1)S(1)}, bf16[512,256]{1,0:T(8,128)(2,1)}, u32[]{:S(2)}) copy-start(bf16[512,256]{1,0:T(8,128)(2,1)} %param.18) | copy-start | bytes 786436
  7.2 71.8 %all-gather.6.cloned.1.call-start = ((), (), s32[]{:S(2)}) async-start(), calls=%async_computation.7 | async-start | bytes 1310720 | tf_op jit(solution)/shard_map/all_gather | solution.py:121
  8.7 4.4 %copy-start.25 = (s32[256,1]{0,1:T(1,128)}, s32[256,1]{0,1:T(1,128)S(1)}, u32[]{:S(2)}) copy-start(s32[256,1]{0,1:T(1,128)S(1)} %get-tuple-element.84) | copy-start | bytes 3076
  8.7 13.2 %copy-start.24 = (s32[256,1]{0,1:T(1,128)}, s32[256,1]{0,1:T(1,128)S(1)}, u32[]{:S(2)}) copy-start(s32[256,1]{0,1:T(1,128)S(1)} %get-tuple-element.85) | copy-start | bytes 3076
  8.7 34.2 %copy-start.23 = (s32[256,1]{0,1:T(1,128)}, s32[256,1]{0,1:T(1,128)S(1)}, u32[]{:S(2)}) copy-start(s32[256,1]{0,1:T(1,128)S(1)} %get-tuple-element.83) | copy-start | bytes 3076
  13.1 14.4 %all-to-all-start.2 = ((bf16[32,2,128]{2,1,0:T(2,128)(2,1)}), bf16[32,2,128]{2,1,0:T(2,128)(2,1)S(1)}, u32[]{:S(2)}, u32[]{:S(2)}) async-start(bf16[32,2,128]{2,1,0:T(2,128)(2,1)} %reshape.345), calls=%async_computation.2 | async-start | bytes 32768 | tf_op jit(solution)/shard_map/all_to_all | solution.py:97
  27.5 12.2 %all-to-all-start.1 = ((bf16[32,8,128]{2,1,0:T(8,128)(2,1)}), bf16[32,8,128]{2,1,0:T(8,128)(2,1)S(1)}, u32[]{:S(2)}, u32[]{:S(2)}) async-start(bf16[32,8,128]{2,1,0:T(8,128)(2,1)} %bitcast.9), calls=%async_computation.1 | async-start | bytes 131072 | tf_op jit(solution)/shard_map/all_to_all | solution.py:90
  39.6 13.3 %copy-start.13 = (bf16[32,8,128]{2,1,0:T(8,128)(2,1)}, bf16[32,8,128]{2,1,0:T(8,128)(2,1)S(1)}, u32[]{:S(2)}) copy-start(bf16[32,8,128]{2,1,0:T(8,128)(2,1)S(1)} %all-to-all-done.1) | copy-start | bytes 196612
  39.7 13.0 %all-to-all-start = ((bf16[32,8,512]{2,1,0:T(8,128)(2,1)}), bf16[32,8,512]{2,1,0:T(8,128)(2,1)S(1)}, u32[]{:S(2)}, u32[]{:S(2)}) async-start(bf16[32,8,512]{2,1,0:T(8,128)(2,1)} %bitcast.5), calls=%async_computation | async-start | bytes 524288 | tf_op jit(solution)/shard_map/all_to_all | solution.py:89
  42.2 221.1 %all-reduce.5.cloned.1.call-start = ((), (), s32[]{:S(2)}) async-start(), calls=%async_computation.9 | async-start | bytes 5505024 | tf_op jit(solution)/shard_map/psum | solution.py:212
  48.1 38.7 %copy-start.18 = (s32[4,1,512]{2,1,0:T(1,128)}, s32[4,1,512]{2,1,0:T(1,128)S(1)}, u32[]{:S(2)}) copy-start(s32[4,1,512]{2,1,0:T(1,128)S(1)} %all-gather.3) | copy-start | bytes 24580
  48.2 4.7 %copy-start.11 = (bf16[256,32]{1,0:T(8,128)(2,1)}, bf16[256,32]{1,0:T(8,128)(2,1)S(1)}, u32[]{:S(2)}) copy-start(bf16[256,32]{1,0:T(8,128)(2,1)S(1)} %reshape.346) | copy-start | bytes 49156
  52.7 0.7 copy-start.6
  72.5 5.8 %copy-start.14 = (bf16[1024,256]{1,0:T(8,128)(2,1)S(1)}, bf16[1024,256]{1,0:T(8,128)(2,1)}, u32[]{:S(2)}) copy-start(bf16[1024,256]{1,0:T(8,128)(2,1)} %param.22) | copy-start | bytes 1572868
  76.9 1.3 copy-start.2
  81.6 7.9 %copy-start.1 = (f32[1024,2048]{1,0:T(8,128)}, f32[1024,2048]{1,0:T(8,128)S(1)}, u32[]{:S(2)}) copy-start(f32[1024,2048]{1,0:T(8,128)S(1)} %get-tuple-element.93) | copy-start | bytes 25165828
  100.5 4.8 %copy-start.19 = (f32[2048]{0:T(1024)}, f32[2048]{0:T(1024)S(1)}, u32[]{:S(2)}) copy-start(f32[2048]{0:T(1024)S(1)} %log_add_fusion) | copy-start | bytes 24580
  100.5 4.8 %copy-start.8 = (bf16[2048,256]{1,0:T(8,128)(2,1)S(1)}, bf16[2048,256]{1,0:T(8,128)(2,1)}, u32[]{:S(2)}) copy-start(bf16[2048,256]{1,0:T(8,128)(2,1)} %all-gather.6.cloned.1.call-done) | copy-start | bytes 3145732
  105.3 2.1 copy-start.5
  105.3 3.7 %copy-start.27 = (f32[1024,1024]{1,0:T(8,128)S(1)}, f32[1024,1024]{1,0:T(8,128)}, u32[]{:S(2)}) copy-start(f32[1024,1024]{1,0:T(8,128)} %get-tuple-element.89) | copy-start | bytes 12582916
  109.0 1.9 copy-start.15
  111.0 1.0 copy-start.4
  111.0 2.7 copy-start.3
  115.4 27.9 %copy-start.7 = (bf16[32,8,512]{2,1,0:T(8,128)(2,1)S(1)}, bf16[32,8,512]{2,1,0:T(8,128)(2,1)}, u32[]{:S(2)}) copy-start(bf16[32,8,512]{2,1,0:T(8,128)(2,1)} %copy-done.6) | copy-start | bytes 786436
  146.2 117.2 %copy-start.21 = (bf16[32,256]{1,0:T(8,128)(2,1)S(1)}, bf16[32,256]{1,0:T(8,128)(2,1)}, u32[]{:S(2)}) copy-start(bf16[32,256]{1,0:T(8,128)(2,1)} %param.20) | copy-start | bytes 49156
  146.2 202.0 %reduce-scatter.2.cloned.1.call-start = ((), (), s32[]{:S(2)}) async-start(), calls=%async_computation.8 | async-start | bytes 1310720 | tf_op jit(solution)/shard_map/reduce_scatter | solution.py:143
  150.8 117.2 %copy-start.17 = (bf16[128,256]{1,0:T(8,128)(2,1)S(1)}, bf16[128,256]{1,0:T(8,128)(2,1)}, u32[]{:S(2)}) copy-start(bf16[128,256]{1,0:T(8,128)(2,1)} %param.19) | copy-start | bytes 196612
  150.8 126.8 %copy-start.10 = (bf16[512,256]{1,0:T(8,128)(2,1)S(1)}, bf16[512,256]{1,0:T(8,128)(2,1)}, u32[]{:S(2)}) copy-start(bf16[512,256]{1,0:T(8,128)(2,1)} %param.18) | copy-start | bytes 786436
  150.8 136.8 %copy-start.12 = (bf16[256,32]{1,0:T(8,128)(2,1)S(1)}, bf16[256,32]{1,0:T(8,128)(2,1)}, u32[]{:S(2)}) copy-start(bf16[256,32]{1,0:T(8,128)(2,1)} %copy-done.11) | copy-start | bytes 49156
  150.8 187.7 %copy-start.22 = (f32[256,4]{0,1:T(4,128)S(1)}, f32[256,4]{0,1:T(4,128)}, u32[]{:S(2)}) copy-start(f32[256,4]{0,1:T(4,128)} %get-tuple-element.86) | copy-start | bytes 12292
  150.8 203.7 %all-reduce.7.cloned.1.call-start = ((), (), s32[]{:S(2)}) async-start(), calls=%async_computation.10 | async-start | bytes 5505024 | tf_op jit(solution)/shard_map/psum | solution.py:211
  264.4 10.7 %all-to-all-start.5 = ((bf16[32,2,128]{2,1,0:T(2,128)(2,1)}), bf16[32,2,128]{2,1,0:T(2,128)(2,1)S(1)}, u32[]{:S(2)}, u32[]{:S(2)}) async-start(bf16[32,2,128]{2,1,0:T(2,128)(2,1)} %convert_element_type.98), calls=%async_computation.6 | async-start | bytes 32768 | tf_op jit(solution)/shard_map/all_to_all | solution.py:189
  275.0 10.0 %all-to-all-start.4 = ((bf16[32,8,128]{2,1,0:T(8,128)(2,1)}), bf16[32,8,128]{2,1,0:T(8,128)(2,1)S(1)}, u32[]{:S(2)}, u32[]{:S(2)}) async-start(bf16[32,8,128]{2,1,0:T(8,128)(2,1)} %fusion.10), calls=%async_computation.5 | async-start | bytes 131072 | tf_op jit(solution)/shard_map/all_to_all | solution.py:180
  285.0 59.6 %all-to-all-start.3 = ((bf16[32,8,512]{2,1,0:T(8,128)(2,1)}), bf16[32,8,512]{2,1,0:T(8,128)(2,1)S(1)}, u32[]{:S(2)}, u32[]{:S(2)}) async-start(bf16[32,8,512]{2,1,0:T(8,128)(2,1)} %fusion.9), calls=%async_computation.4 | async-start | bytes 524288 | tf_op jit(solution)/shard_map/all_to_all | solution.py:171
Sparse Core Ops, SparseCore 0:
  9.6 19.5 all-gather.5
  146.3 116.9 all-reduce.4
  265.8 24.0 reduce-scatter.1
  292.4 62.0 all-reduce.6
